TPU v7x, 32 devices: a whole 2x2x4 slice. The times are simulated.
32 devices in a mesh: replica: 2 (over x), tp: 8 (over z, y), sub: 2 (over core).
Axes of the slice: x: 2, y: 2, z: 4, core: 2. Of those that a mesh axis runs over, the one named last changes fastest.
Arguments:
- hidden_in: bfloat16 [8, 8192], P('replica'), parts along dimension 0, may hold values from -6 to 6
- norm_gain: float32 [16384], P('replica'), parts along dimension 0, may hold values from 0.1 to 1.9
- wqkv_old: bfloat16 [16, 2, 1280, 4096], P(('replica', 'tp'), 'sub'), parts along dimension 0, may hold values from -0.1875 to 0.1875
- wo: bfloat16 [16384, 8192], P(('replica', 'tp', 'sub')), parts along dimension 0, may hold values from -0.0625 to 0.0625
- key_cache: bfloat16 [8, 4096, 1024], P('replica', ('tp', 'sub')), parts along dimension 0, may hold values from -240 to 240
- value_cache: bfloat16 [8, 4096, 1024], P('replica', ('tp', 'sub')), parts along dimension 0, may hold values from -6 to 6
- lengths: int32 [8], P('replica'), parts along dimension 0, may hold values from 1 to 4096
- section_order: int32 [32], P('replica'), parts along dimension 0, may hold values from 0 to 15, each once
Outputs:
- mixed_out: bfloat16 [8, 8192], P('replica'), parts along dimension 0
- wqkv_new: bfloat16 [16, 2, 640, 8192], P(('replica', 'tp'), 'sub'), parts along dimension 0
There are 2 independent parts, one for each index of `replica`. A program takes and returns all parts, laid end to end along the dimension named above; each array names one. Nothing has to cross between parts.
Inputs may be any that keep to these rules, and one draw needn't show every extreme that they name: `section_order`: each input row block appears once. The new token's position is lengths[b].
All inputs are finite; a program needn't handle non-finite values.
Results may differ from a plain program's by a relative error of at most 0.0085.
The roundings to bfloat16 on the way count: a program that leaves them out, or rounds other values in their place, can miss the bound.
Values may be sent and summed in bfloat16 or wider, within the bound.
A program may use at most 128 MiB of HBM per device.

v0:
```python
import math
import jax
import jax.numpy as jnp
from jax import lax
from jax.sharding import PartitionSpec as P

HEADS = 64
KV_HEADS = 8
HEAD_DIM = 128
RANKS = 8
ROW_BLOCKS = 16


def passed_along(value, axis, steps):
    count = lax.axis_size(axis)
    pairs = [(source, (source + steps) % count) for source in range(count)]
    return lax.ppermute(value, axis, pairs)


def rotary(values, positions):
    half = values.shape[-1] // 2
    freqs = 500000.0 ** (-jnp.arange(half, dtype=jnp.float32) * 2.0 / values.shape[-1])
    angles = positions.astype(jnp.float32)[:, None] * freqs[None, :]
    cosine = jnp.cos(angles)[:, None, :]
    sine = jnp.sin(angles)[:, None, :]
    first_half = values[..., :half]
    second_half = values[..., half:]
    return jnp.concatenate(
        [first_half * cosine - second_half * sine, second_half * cosine + first_half * sine], -1
    )


def rms_normed(hidden_in, norm_gain):
    widened = hidden_in.astype(jnp.float32)
    factor = lax.rsqrt(jnp.mean(widened * widened, -1, keepdims=True) + 1e-05)
    return (widened, (widened * factor * norm_gain).astype(jnp.bfloat16))


def shards(hidden_in, norm_gain, wqkv_old, wo, key_cache, value_cache, lengths, section_order):
    tp_count = lax.axis_size("tp")
    section_count = tp_count // 4
    per_section = ROW_BLOCKS // section_count
    tp_index = lax.axis_index("tp")
    sub_index = lax.axis_index("sub")
    own_section = tp_index // 4
    device_rank = tp_index * 2 + sub_index
    cols_dev = wqkv_old.shape[2] // section_count
    rows_old = wqkv_old.shape[3]
    block_rows = rows_old // per_section
    old_block = wqkv_old[0, 0].reshape(section_count, cols_dev, rows_old)
    slot_ids = jnp.arange(section_count, dtype=jnp.int32)
    arrived = [lax.dynamic_index_in_dim(old_block, own_section, 0, keepdims=False)]
    for offset in range(1, section_count):
        outgoing = lax.dynamic_index_in_dim(
            old_block, (own_section + offset) % section_count, 0, keepdims=False
        )
        arrived.append(passed_along(outgoing, "tp", 4 * offset))
    received = jnp.stack(arrived, 0)
    sources = (own_section - slot_ids) % section_count
    block_ids = jnp.arange(ROW_BLOCKS, dtype=jnp.int32)
    local_source = (
        sources[:, None] * per_section + jnp.arange(per_section, dtype=jnp.int32)[None, :]
    ).reshape(ROW_BLOCKS)
    target_block = jnp.take(section_order, local_source, axis=0)
    placing = (target_block[None, :] == block_ids[:, None]).astype(jnp.bfloat16)
    received_blocks = jnp.transpose(
        received.reshape(section_count, cols_dev, per_section, block_rows), (0, 2, 1, 3)
    ).reshape(ROW_BLOCKS, cols_dev, block_rows)
    new_weight = jnp.einsum(
        "sa,acr->csr", placing, received_blocks, preferred_element_type=jnp.float32
    ).astype(jnp.bfloat16)
    new_weight = new_weight.reshape(cols_dev, ROW_BLOCKS * block_rows)
    widened, normed = rms_normed(hidden_in, norm_gain)
    projected = lax.dot_general(
        normed, new_weight, (((1,), (1,)), ((), ())), preferred_element_type=jnp.float32
    ).astype(jnp.bfloat16)
    gathered = lax.all_gather(projected[:, None, :], ("tp", "sub"), axis=1, tiled=True)
    seq_count = hidden_in.shape[0]
    projected_all = jnp.transpose(
        gathered.reshape(seq_count, section_count, RANKS, cols_dev), (0, 2, 1, 3)
    ).reshape(seq_count, -1)
    q_width = HEADS * HEAD_DIM
    kv_width = KV_HEADS * HEAD_DIM
    groups = HEADS // KV_HEADS
    queries = rotary(
        projected_all[:, :q_width].astype(jnp.float32).reshape(seq_count, HEADS, HEAD_DIM), lengths
    ).astype(jnp.bfloat16)
    new_keys = rotary(
        projected_all[:, q_width : q_width + kv_width]
        .astype(jnp.float32)
        .reshape(seq_count, KV_HEADS, HEAD_DIM),
        lengths,
    ).astype(jnp.bfloat16)
    new_values = (
        projected_all[:, q_width + kv_width :]
        .astype(jnp.float32)
        .reshape(seq_count, KV_HEADS, HEAD_DIM)
    )
    pos_count = key_cache.shape[1]
    positions = device_rank * pos_count + jnp.arange(pos_count, dtype=jnp.int32)
    usable = (positions[None, :] < lengths[:, None])[:, None, None, :]
    inverse = 1.0 / math.sqrt(HEAD_DIM)
    grouped = queries.reshape(seq_count, KV_HEADS, groups, HEAD_DIM)
    keys_local = key_cache.reshape(seq_count, pos_count, KV_HEADS, HEAD_DIM)
    values_local = value_cache.reshape(seq_count, pos_count, KV_HEADS, HEAD_DIM).astype(jnp.float32)
    scores = (
        jnp.einsum("bkgd,bpkd->bkgp", grouped, keys_local, preferred_element_type=jnp.float32)
        * inverse
    )
    local_top = jnp.max(jnp.where(usable, scores, -1e30), -1)
    weights = jnp.exp(jnp.where(usable, scores - local_top[..., None], -1e30))
    local_sum = jnp.sum(weights, -1).reshape(seq_count, HEADS)
    local_mix = jnp.einsum("bkgp,bpkd->bkgd", weights, values_local).reshape(
        seq_count, HEADS, HEAD_DIM
    )
    local_top = local_top.reshape(seq_count, HEADS)
    heads_dev = wo.shape[0] // HEAD_DIM
    first_head = device_rank * heads_dev
    tops_in, sums_in, mixes_in = (
        lax.all_to_all(local_top[None], ("tp", "sub"), split_axis=2, concat_axis=0, tiled=True),
        lax.all_to_all(local_sum[None], ("tp", "sub"), split_axis=2, concat_axis=0, tiled=True),
        lax.all_to_all(local_mix[None], ("tp", "sub"), split_axis=2, concat_axis=0, tiled=True),
    )
    best = jnp.max(tops_in, 0)
    factors = jnp.exp(tops_in - best[None])
    head_sum = jnp.sum(sums_in * factors, 0)
    head_mix = jnp.sum(mixes_in * factors[..., None], 0)
    own_queries = lax.dynamic_slice_in_dim(queries, first_head, heads_dev, 1).astype(jnp.float32)
    kv_index = (first_head + jnp.arange(heads_dev, dtype=jnp.int32)) // groups
    own_keys = jnp.take(new_keys, kv_index, axis=1).astype(jnp.float32)
    own_values = jnp.take(new_values, kv_index, axis=1)
    own_score = jnp.sum(own_queries * own_keys, -1) * inverse
    highest = jnp.maximum(best, own_score)
    old_scale = jnp.exp(best - highest)
    own_weight = jnp.exp(own_score - highest)
    numerator = head_mix * old_scale[..., None] + own_weight[..., None] * own_values
    denominator = head_sum * old_scale + own_weight
    attended = (
        (numerator / denominator[..., None])
        .reshape(seq_count, heads_dev * HEAD_DIM)
        .astype(jnp.bfloat16)
    )
    partial_out = jnp.dot(attended, wo, preferred_element_type=jnp.float32)
    summed_out = lax.psum(partial_out, ("tp", "sub"))
    mixed_out = (widened + summed_out).astype(jnp.bfloat16)
    return (mixed_out, new_weight[None, None])


def solution(mesh):
    placed = (
        P("replica", None),
        P("replica"),
        P(("replica", "tp"), "sub", None, None),
        P(("replica", "tp", "sub"), None),
        P("replica", ("tp", "sub"), None),
        P("replica", ("tp", "sub"), None),
        P("replica"),
        P("replica"),
    )
    return jax.shard_map(
        shards,
        mesh=mesh,
        in_specs=placed,
        out_specs=(P("replica", None), P(("replica", "tp"), "sub", None, None)),
        check_vma=False,
    )
```

profile of v0, /device:TPU:8, one launch (start us, length us, event | category | flops | bytes accessed | tf_op | source)
XLA Modules:
  0.0 444.4 jit_solution(11691780571699023312)
XLA Ops:
  7.2 9.9 %constant_dynamic-slice_fusion = (bf16[1,640,4096]{2,1,0:T(8,128)(2,1)}, bf16[640,4096]{1,0:T(8,128)(2,1)}) fusion(bf16[2,640,4096]{2,1,0:T(8,128)(2,1)} %bitcast.145, s32[]{:T(128)S(6)} %select_n.109, s32[]{:T(128)S(6)} %select_n.111), kind=kLoop, calls=%fused_computation.104 | loop fusion | bytes 20971528 | tf_op jit(solution)/shard_map/jit(dynamic_index_in_dim)/dynamic_slice | solution.py:52
  17.1 2.6 collective-permute-start
  19.9 8.3 %copy.49 = bf16[80,8,8,512]{3,2,1,0:T(8,128)(2,1)} copy(bf16[80,8,8,512]{3,1,2,0:T(8,128)(2,1)} %bitcast.144) | data formatting | bytes 10485760
  29.5 215.0 %collective-permute-done = bf16[640,4096]{1,0:T(8,128)(2,1)} collective-permute-done((bf16[640,4096]{1,0:T(8,128)(2,1)}, bf16[640,4096]{1,0:T(8,128)(2,1)}, u32[]{:S(2)}, u32[]{:S(2)}) %collective-permute-start) | collective-permute-done | bytes 5242912 | tf_op jit(solution)/shard_map/ppermute | solution.py:17
  244.5 6.1 %copy.50 = bf16[80,8,8,512]{3,2,1,0:T(8,128)(2,1)S(1)} copy(bf16[80,8,8,512]{3,1,2,0:T(8,128)(2,1)} %bitcast.49) | data formatting | bytes 10485760
  250.7 5.6 %fusion.3 = bf16[640,512,16]{1,2,0:T(8,128)(2,1)} fusion(bf16[1,640,8,512]{3,2,0,1:T(8,128)(2,1)S(1)} %bitcast.149, bf16[1,640,8,512]{3,2,0,1:T(8,128)(2,1)S(1)} %bitcast.148, s32[16]{0:T(128)S(1)} %and_select_fusion.2), kind=kOutput, calls=%fused_computation.7 | convolution fusion | flops 178258176 | bytes 20971584 | tf_op jit(solution)/shard_map/sa,acr->csr/dot_general | solution.py:69
  256.3 20.5 %copy.51 = bf16[80,8,16,512]{3,1,2,0:T(8,128)(2,1)} copy(bf16[80,8,16,512]{3,2,1,0:T(8,128)(2,1)} %bitcast.141) | data formatting | bytes 20971520
  276.8 6.8 %convolution_convert_fusion = bf16[4,640]{1,0:T(4,128)(2,1)S(1)} fusion(bf16[640,8192]{1,0:T(8,128)(2,1)} %bitcast.143, bf16[4,8192]{1,0:T(4,128)(2,1)S(1)} %copy-done.2, f32[8192]{0:T(1024)S(1)} %copy-done.3, f32[4]{0:T(128)S(1)} %add_rsqrt_fusion), kind=kOutput, calls=%fused_computation.17 | convolution fusion | flops 42076672 | bytes 10589200 | tf_op jit(solution)/shard_map/dot_general | solution.py:74
  283.6 19.8 %all-gather = bf16[4,10240]{1,0:T(4,128)(2,1)S(1)} all-gather(bf16[4,640]{1,0:T(4,128)(2,1)S(1)} %convolution_convert_fusion), channel_id=2, replica_groups=mesh['replica'=2,'tp'=8,'sub'=2] {'tp','sub'}, dimensions={1}, use_global_device_ids=true | all-gather | bytes 87040 | tf_op jit(solution)/shard_map/all_gather | solution.py:77
  303.8 0.8 select_reduce_fusion
  304.8 2.0 fusion.13
  306.8 0.7 copy.45
  307.6 6.6 %all-to-all-start.2 = ((f32[1,4,64]{1,0,2:T(1,128)}), f32[1,4,64]{1,0,2:T(1,128)S(1)}, u32[]{:S(2)}, u32[]{:S(2)}) async-start(f32[1,4,64]{1,0,2:T(1,128)} %bitcast.29), calls=%async_computation.2 | async-start | bytes 65536 | tf_op jit(solution)/shard_map/all_to_all | solution.py:121
  314.3 0.7 copy.37
  315.6 3.6 all-to-all-done.2
  319.3 5.0 %all-to-all-start.1 = ((f32[1,4,64]{1,0,2:T(1,128)}), f32[1,4,64]{1,0,2:T(1,128)S(1)}, u32[]{:S(2)}, u32[]{:S(2)}) async-start(f32[1,4,64]{1,0,2:T(1,128)} %bitcast.16), calls=%async_computation.1 | async-start | bytes 65536 | tf_op jit(solution)/shard_map/all_to_all | solution.py:120
  324.4 0.7 copy.36
  326.0 3.3 all-to-all-done.1
  329.4 5.0 %all-to-all-start = ((f32[1,4,64,128]{3,1,0,2:T(4,128)}), f32[1,4,64,128]{3,1,0,2:T(4,128)S(1)}, u32[]{:S(2)}, u32[]{:S(2)}) async-start(f32[1,4,64,128]{3,1,0,2:T(4,128)} %copy.36), calls=%async_computation | async-start | bytes 262144 | tf_op jit(solution)/shard_map/all_to_all | solution.py:122
  335.1 4.7 %all-to-all-done = f32[1,4,64,128]{3,1,0,2:T(4,128)S(1)} async-done(((f32[1,4,64,128]{3,1,0,2:T(4,128)}), f32[1,4,64,128]{3,1,0,2:T(4,128)S(1)}, u32[]{:S(2)}, u32[]{:S(2)}) %all-to-all-start) | async-done | bytes 131104 | tf_op jit(solution)/shard_map/all_to_all | solution.py:122
  339.9 5.3 %fusion.41 = f32[4,8192]{1,0:T(4,128)} fusion(bf16[512,8192]{1,0:T(8,128)(2,1)} %param.11, f32[1,4,4,128]{3,2,1,0:T(4,128)S(1)} %broadcast_bitcast_fusion, f32[4,4,128]{2,1,0:T(4,128)S(1)} %gather_fusion.2, f32[1,4,4,128]{3,2,1,0:T(4,128)S(1)} %broadcast_bitcast_fusion.1, f32[4,4,128]{2,0,1:T(4,128)S(1)} %multiply_reduce_fusion, f32[4,4]{0,1:T(4,128)S(1)} %copy.41, ...), kind=kOutput, calls=%fused_computation.69 | convolution fusion | flops 33566720 | bytes 8553024 | tf_op jit(solution)/shard_map/dot_general | solution.py:143
  345.2 16.5 %broadcast_in_dim_reshape.15 = bf16[1,1,640,8192]{3,2,1,0:T(8,128)(2,1)} reshape(bf16[640,16,512]{2,1,0:T(8,128)(2,1)} %bitcast.142) | data formatting | bytes 20971520 | tf_op jit(solution)/shard_map/broadcast_in_dim;reshape | solution.py:146
  361.7 74.2 %all-reduce.2.cloned.1.call-done = f32[4,8192]{1,0:T(4,128)} async-done(((f32[4,8192]{1,0:T(4,128)}), f32[4,8192]{1,0:T(4,128)}) %all-reduce.2.cloned.1.call-update) | async-done | bytes 131088 | tf_op jit(solution)/shard_map/psum | solution.py:144
  435.9 1.6 fusion.20
  (60 shorter events, 4.7 us)
Async XLA Ops:
  7.2 296.6 %copy-start = (bf16[4,256,1024]{2,1,0:T(8,128)(2,1)S(1)}, bf16[4,256,1024]{2,1,0:T(8,128)(2,1)}, u32[]{:S(2)}) copy-start(bf16[4,256,1024]{2,1,0:T(8,128)(2,1)} %param.12) | copy-start | bytes 6291460
  17.1 227.4 %collective-permute-start = (bf16[640,4096]{1,0:T(8,128)(2,1)}, bf16[640,4096]{1,0:T(8,128)(2,1)}, u32[]{:S(2)}, u32[]{:S(2)}) collective-permute-start(bf16[640,4096]{1,0:T(8,128)(2,1)} %get-tuple-element.8), channel_id=1, source_target_pairs={{0,8},{2,10},{4,12},{6,14},{8,0},{10,2},{12,4},{14,6},{1,9},{3,11}... | collective-permute-start | bytes 15728648 | tf_op jit(solution)/shard_map/ppermute | solution.py:17
  19.9 8.4 %copy-start.4 = (s32[4]{0:T(128)S(1)}, s32[4]{0:T(128)}, u32[]{:S(2)}) copy-start(s32[4]{0:T(128)} %param.14) | copy-start | bytes 52
  19.9 8.4 %copy-start.1 = (s32[16]{0:T(128)S(1)}, s32[16]{0:T(128)}, u32[]{:S(2)}) copy-start(s32[16]{0:T(128)} %param.15) | copy-start | bytes 196
  19.9 9.1 %copy-start.2 = (bf16[4,8192]{1,0:T(4,128)(2,1)S(1)}, bf16[4,8192]{1,0:T(4,128)(2,1)}, u32[]{:S(2)}) copy-start(bf16[4,8192]{1,0:T(4,128)(2,1)} %param.8) | copy-start | bytes 196612
  28.3 222.4 %slice-start = ((s8[5242880]{0:T(1024)(128)(4,1)}), s8[1048576]{0:T(1024)(128)(4,1)S(1)}, s32[]{:S(2)}) async-start(s8[5242880]{0:T(1024)(128)(4,1)} %bitcast.146), calls=%async_computation.4 | async-start | bytes 2097152
  244.5 6.1 %slice-start.1 = ((s8[5242880]{0:T(1024)(128)(4,1)}), s8[4194304]{0:T(1024)(128)(4,1)S(1)}, s32[]{:S(2)}) async-start(s8[5242880]{0:T(1024)(128)(4,1)} %bitcast.146), calls=%async_computation.5 | async-start | bytes 8388608
  256.3 20.6 %copy-start.3 = (f32[8192]{0:T(1024)S(1)}, f32[8192]{0:T(1024)}, u32[]{:S(2)}) copy-start(f32[8192]{0:T(1024)} %param.9) | copy-start | bytes 98308
  307.6 11.7 %all-to-all-start.2 = ((f32[1,4,64]{1,0,2:T(1,128)}), f32[1,4,64]{1,0,2:T(1,128)S(1)}, u32[]{:S(2)}, u32[]{:S(2)}) async-start(f32[1,4,64]{1,0,2:T(1,128)} %bitcast.29), calls=%async_computation.2 | async-start | bytes 65536 | tf_op jit(solution)/shard_map/all_to_all | solution.py:121
  319.3 10.1 %all-to-all-start.1 = ((f32[1,4,64]{1,0,2:T(1,128)}), f32[1,4,64]{1,0,2:T(1,128)S(1)}, u32[]{:S(2)}, u32[]{:S(2)}) async-start(f32[1,4,64]{1,0,2:T(1,128)} %bitcast.16), calls=%async_computation.1 | async-start | bytes 65536 | tf_op jit(solution)/shard_map/all_to_all | solution.py:120
  329.4 10.4 %all-to-all-start = ((f32[1,4,64,128]{3,1,0,2:T(4,128)}), f32[1,4,64,128]{3,1,0,2:T(4,128)S(1)}, u32[]{:S(2)}, u32[]{:S(2)}) async-start(f32[1,4,64,128]{3,1,0,2:T(4,128)} %copy.36), calls=%async_computation | async-start | bytes 262144 | tf_op jit(solution)/shard_map/all_to_all | solution.py:122
  334.4 101.6 %all-reduce.2.cloned.1.call-start = ((), (), s32[]{:S(2)}) async-start(), calls=%async_computation.3 | async-start | bytes 262144 | tf_op jit(solution)/shard_map/psum | solution.py:144
Sparse Core Ops, SparseCore 0:
  345.4 90.5 all-reduce.1
where the time goes:
time: 445 us; the launch traced here: 444 us
  waiting for transfers between devices  301 us (68%)
  local copies, waits for them, and re-layouts  66.7 us (15%)
  matrix products  20.4 us (5%)
  blocking collectives  19.8 us (4%)
  starting transfers between devices  19.2 us (4%)
  between operations  14.3 us (3%)
    ppermute x1, waiting for transfers between devices, passed_along(): return lax.ppermute(value, axis, pairs)  215 us
    psum x1, waiting for transfers between devices, shards(): summed_out = lax.psum(partial_out, ('tp', 'sub'))  74.2 us
    unnamed x20, local copies, waits for them, and re-layouts  35.2 us
    all_gather x1, blocking collectives, shards(): lax.all_gather(projected[:, None, :], ('tp', 'sub'), axis=1, tiled=True)  19.8 us
    another operation x1, local copies, waits for them, and re-layouts, shards(): return (mixed_out, new_weight[None, None])  16.5 us
    dynamic_slice x1, local copies, waits for them, and re-layouts, shards(): lax.dynamic_index_in_dim(old_block, own_section, 0, keepdims=False)  9.85 us
  transfers between devices with their start and end apart: 5, of which 5 were waited for; matrix products, arithmetic and copies ran while one was open for 7% of the time, Pallas kernels for 0%

commit v1 on v0

--- a/solution.py
+++ b/solution.py
@@ -141,7 +141,8 @@
         .astype(jnp.bfloat16)
     )
     partial_out = jnp.dot(attended, wo, preferred_element_type=jnp.float32)
-    summed_out = lax.psum(partial_out, ("tp", "sub"))
+    side_arr = lax.all_gather(partial_out, ("tp", "sub"))
+    summed_out = jnp.sum(side_arr, axis=0)
     mixed_out = (widened + summed_out).astype(jnp.bfloat16)
     return (mixed_out, new_weight[None, None])
 

time: 445 us -> 399 us (0.90)
  waiting for transfers between devices: 301 us -> 250 us
    psum x1 -> x0, waiting for transfers between devices: 74.2 us -> none  [shards(): summed_out = lax.psum(partial_out, ('tp', 'sub'))]
    all_gather x0 -> x1, waiting for transfers between devices: none -> 23.7 us  [shards(): side_arr = lax.all_gather(partial_out, ('tp', 'sub'))]
  transfers between devices with their start and end apart: 5 -> 5, of which waited for: 5 -> 5; matrix products, arithmetic and copies ran while one was open for 7% -> 8% of each run, Pallas kernels for 0% -> 0%
where the time goes in v1:
time: 399 us; the launch traced here: 395 us
  waiting for transfers between devices  250 us (63%)
  local copies, waits for them, and re-layouts  66.8 us (17%)
  matrix products  20.4 us (5%)
  blocking collectives  19.8 us (5%)
  starting transfers between devices  19.2 us (5%)
  between operations  14.3 us (4%)
  other arithmetic  4.04 us (1%)
    ppermute x1, waiting for transfers between devices, passed_along(): return lax.ppermute(value, axis, pairs)  215 us
    unnamed x20, local copies, waits for them, and re-layouts  35.2 us
    all_gather x1, waiting for transfers between devices, shards(): side_arr = lax.all_gather(partial_out, ('tp', 'sub'))  23.7 us
    all_gather x1, blocking collectives, shards(): lax.all_gather(projected[:, None, :], ('tp', 'sub'), axis=1, tiled=True)  19.8 us
    another operation x1, local copies, waits for them, and re-layouts, shards(): return (mixed_out, new_weight[None, None])  16.5 us
    dynamic_slice x1, local copies, waits for them, and re-layouts, shards(): lax.dynamic_index_in_dim(old_block, own_section, 0, keepdims=False)  9.85 us
  transfers between devices with their start and end apart: 5, of which 5 were waited for; matrix products, arithmetic and copies ran while one was open for 8% of the time, Pallas kernels for 0%

profile of v1, /device:TPU:8, one launch (start us, length us, event | category | flops | bytes accessed | tf_op | source)
XLA Modules:
  0.0 394.9 jit_solution(15745159634802425812)
XLA Ops:
  7.2 9.9 %constant_dynamic-slice_fusion = (bf16[1,640,4096]{2,1,0:T(8,128)(2,1)}, bf16[640,4096]{1,0:T(8,128)(2,1)}) fusion(bf16[2,640,4096]{2,1,0:T(8,128)(2,1)} %bitcast.147, s32[]{:T(128)S(6)} %select_n.109, s32[]{:T(128)S(6)} %select_n.111), kind=kLoop, calls=%fused_computation.104 | loop fusion | bytes 20971528 | tf_op jit(solution)/shard_map/jit(dynamic_index_in_dim)/dynamic_slice | solution.py:52
  17.1 2.6 collective-permute-start
  19.9 8.3 %copy.49 = bf16[80,8,8,512]{3,2,1,0:T(8,128)(2,1)} copy(bf16[80,8,8,512]{3,1,2,0:T(8,128)(2,1)} %bitcast.146) | data formatting | bytes 10485760
  29.5 215.0 %collective-permute-done = bf16[640,4096]{1,0:T(8,128)(2,1)} collective-permute-done((bf16[640,4096]{1,0:T(8,128)(2,1)}, bf16[640,4096]{1,0:T(8,128)(2,1)}, u32[]{:S(2)}, u32[]{:S(2)}) %collective-permute-start) | collective-permute-done | bytes 5242912 | tf_op jit(solution)/shard_map/ppermute | solution.py:17
  244.5 6.1 %copy.50 = bf16[80,8,8,512]{3,2,1,0:T(8,128)(2,1)S(1)} copy(bf16[80,8,8,512]{3,1,2,0:T(8,128)(2,1)} %bitcast.50) | data formatting | bytes 10485760
  250.7 5.6 %fusion.3 = bf16[640,512,16]{1,2,0:T(8,128)(2,1)} fusion(bf16[1,640,8,512]{3,2,0,1:T(8,128)(2,1)S(1)} %bitcast.151, bf16[1,640,8,512]{3,2,0,1:T(8,128)(2,1)S(1)} %bitcast.150, s32[16]{0:T(128)S(1)} %and_select_fusion.2), kind=kOutput, calls=%fused_computation.8 | convolution fusion | flops 178258176 | bytes 20971584 | tf_op jit(solution)/shard_map/sa,acr->csr/dot_general | solution.py:69
  256.3 20.5 %copy.51 = bf16[80,8,16,512]{3,1,2,0:T(8,128)(2,1)} copy(bf16[80,8,16,512]{3,2,1,0:T(8,128)(2,1)} %bitcast.143) | data formatting | bytes 20971520
  276.8 6.8 %convolution_convert_fusion = bf16[4,640]{1,0:T(4,128)(2,1)S(1)} fusion(bf16[640,8192]{1,0:T(8,128)(2,1)} %bitcast.145, bf16[4,8192]{1,0:T(4,128)(2,1)S(1)} %copy-done.2, f32[8192]{0:T(1024)S(1)} %copy-done.3, f32[4]{0:T(128)S(1)} %add_rsqrt_fusion), kind=kOutput, calls=%fused_computation.18 | convolution fusion | flops 42076672 | bytes 10589200 | tf_op jit(solution)/shard_map/dot_general | solution.py:74
  283.6 19.8 %all-gather = bf16[4,10240]{1,0:T(4,128)(2,1)S(1)} all-gather(bf16[4,640]{1,0:T(4,128)(2,1)S(1)} %convolution_convert_fusion), channel_id=2, replica_groups=mesh['replica'=2,'tp'=8,'sub'=2] {'tp','sub'}, dimensions={1}, use_global_device_ids=true | all-gather | bytes 87040 | tf_op jit(solution)/shard_map/all_gather | solution.py:77
  303.8 0.8 select_reduce_fusion
  304.8 2.0 fusion.13
  306.8 0.7 copy.45
  307.6 6.6 %all-to-all-start.2 = ((f32[1,4,64]{1,0,2:T(1,128)}), f32[1,4,64]{1,0,2:T(1,128)S(1)}, u32[]{:S(2)}, u32[]{:S(2)}) async-start(f32[1,4,64]{1,0,2:T(1,128)} %bitcast.29), calls=%async_computation.2 | async-start | bytes 65536 | tf_op jit(solution)/shard_map/all_to_all | solution.py:121
  314.3 0.7 copy.37
  315.6 3.6 all-to-all-done.2
  319.3 5.0 %all-to-all-start.1 = ((f32[1,4,64]{1,0,2:T(1,128)}), f32[1,4,64]{1,0,2:T(1,128)S(1)}, u32[]{:S(2)}, u32[]{:S(2)}) async-start(f32[1,4,64]{1,0,2:T(1,128)} %bitcast.16), calls=%async_computation.1 | async-start | bytes 65536 | tf_op jit(solution)/shard_map/all_to_all | solution.py:120
  324.4 0.7 copy.36
  326.0 3.3 all-to-all-done.1
  329.4 5.0 %all-to-all-start = ((f32[1,4,64,128]{3,1,0,2:T(4,128)}), f32[1,4,64,128]{3,1,0,2:T(4,128)S(1)}, u32[]{:S(2)}, u32[]{:S(2)}) async-start(f32[1,4,64,128]{3,1,0,2:T(4,128)} %copy.36), calls=%async_computation | async-start | bytes 262144 | tf_op jit(solution)/shard_map/all_to_all | solution.py:122
  335.1 4.6 %all-to-all-done = f32[1,4,64,128]{3,1,0,2:T(4,128)S(1)} async-done(((f32[1,4,64,128]{3,1,0,2:T(4,128)}), f32[1,4,64,128]{3,1,0,2:T(4,128)S(1)}, u32[]{:S(2)}, u32[]{:S(2)}) %all-to-all-start) | async-done | bytes 131104 | tf_op jit(solution)/shard_map/all_to_all | solution.py:122
  339.9 5.3 %convolution_bitcast_fusion = f32[1,4,8192]{2,1,0:T(4,128)} fusion(bf16[512,8192]{1,0:T(8,128)(2,1)} %param.11, f32[1,4,4,128]{3,2,1,0:T(4,128)S(1)} %broadcast_bitcast_fusion, f32[4,4,128]{2,1,0:T(4,128)S(1)} %gather_fusion.2, f32[1,4,4,128]{3,2,1,0:T(4,128)S(1)} %broadcast_bitcast_fusion.1, f32[4,4,128]{2,0,1:T(4,128)S(1)} %multiply_reduce_fusion, ...), kind=kOutput, calls=%fused_computation.7 | convolution fusion | flops 33566720 | bytes 8553024 | tf_op jit(solution)/shard_map/dot_general | solution.py:143
  345.2 16.5 %broadcast_in_dim_reshape.15 = bf16[1,1,640,8192]{3,2,1,0:T(8,128)(2,1)} reshape(bf16[640,16,512]{2,1,0:T(8,128)(2,1)} %bitcast.144) | data formatting | bytes 20971520 | tf_op jit(solution)/shard_map/broadcast_in_dim;reshape | solution.py:147
  361.8 23.7 %all-gather.5.cloned.1.call-done = f32[16,4,8192]{2,1,0:T(4,128)} async-done(((f32[1,4,8192]{2,1,0:T(4,128)}), f32[16,4,8192]{2,1,0:T(4,128)}) %all-gather.5.cloned.1.call-update) | async-done | bytes 2097168 | tf_op jit(solution)/shard_map/all_gather | solution.py:144
  385.5 1.9 reduce_sum.59
  (61 shorter events, 5.3 us)
Async XLA Ops:
  7.2 296.6 %copy-start = (bf16[4,256,1024]{2,1,0:T(8,128)(2,1)S(1)}, bf16[4,256,1024]{2,1,0:T(8,128)(2,1)}, u32[]{:S(2)}) copy-start(bf16[4,256,1024]{2,1,0:T(8,128)(2,1)} %param.12) | copy-start | bytes 6291460
  17.1 227.4 %collective-permute-start = (bf16[640,4096]{1,0:T(8,128)(2,1)}, bf16[640,4096]{1,0:T(8,128)(2,1)}, u32[]{:S(2)}, u32[]{:S(2)}) collective-permute-start(bf16[640,4096]{1,0:T(8,128)(2,1)} %get-tuple-element.8), channel_id=1, source_target_pairs={{0,8},{2,10},{4,12},{6,14},{8,0},{10,2},{12,4},{14,6},{1,9},{3,11}... | collective-permute-start | bytes 15728648 | tf_op jit(solution)/shard_map/ppermute | solution.py:17
  19.9 8.4 %copy-start.4 = (s32[4]{0:T(128)S(1)}, s32[4]{0:T(128)}, u32[]{:S(2)}) copy-start(s32[4]{0:T(128)} %param.14) | copy-start | bytes 52
  19.9 8.4 %copy-start.1 = (s32[16]{0:T(128)S(1)}, s32[16]{0:T(128)}, u32[]{:S(2)}) copy-start(s32[16]{0:T(128)} %param.15) | copy-start | bytes 196
  19.9 9.1 %copy-start.2 = (bf16[4,8192]{1,0:T(4,128)(2,1)S(1)}, bf16[4,8192]{1,0:T(4,128)(2,1)}, u32[]{:S(2)}) copy-start(bf16[4,8192]{1,0:T(4,128)(2,1)} %param.8) | copy-start | bytes 196612
  28.3 222.4 %slice-start = ((s8[5242880]{0:T(1024)(128)(4,1)}), s8[1048576]{0:T(1024)(128)(4,1)S(1)}, s32[]{:S(2)}) async-start(s8[5242880]{0:T(1024)(128)(4,1)} %bitcast.148), calls=%async_computation.4 | async-start | bytes 2097152
  244.5 6.1 %slice-start.1 = ((s8[5242880]{0:T(1024)(128)(4,1)}), s8[4194304]{0:T(1024)(128)(4,1)S(1)}, s32[]{:S(2)}) async-start(s8[5242880]{0:T(1024)(128)(4,1)} %bitcast.148), calls=%async_computation.5 | async-start | bytes 8388608
  256.3 20.6 %copy-start.3 = (f32[8192]{0:T(1024)S(1)}, f32[8192]{0:T(1024)}, u32[]{:S(2)}) copy-start(f32[8192]{0:T(1024)} %param.9) | copy-start | bytes 98308
  307.6 11.7 %all-to-all-start.2 = ((f32[1,4,64]{1,0,2:T(1,128)}), f32[1,4,64]{1,0,2:T(1,128)S(1)}, u32[]{:S(2)}, u32[]{:S(2)}) async-start(f32[1,4,64]{1,0,2:T(1,128)} %bitcast.29), calls=%async_computation.2 | async-start | bytes 65536 | tf_op jit(solution)/shard_map/all_to_all | solution.py:121
  319.3 10.1 %all-to-all-start.1 = ((f32[1,4,64]{1,0,2:T(1,128)}), f32[1,4,64]{1,0,2:T(1,128)S(1)}, u32[]{:S(2)}, u32[]{:S(2)}) async-start(f32[1,4,64]{1,0,2:T(1,128)} %bitcast.16), calls=%async_computation.1 | async-start | bytes 65536 | tf_op jit(solution)/shard_map/all_to_all | solution.py:120
  329.4 10.4 %all-to-all-start = ((f32[1,4,64,128]{3,1,0,2:T(4,128)}), f32[1,4,64,128]{3,1,0,2:T(4,128)S(1)}, u32[]{:S(2)}, u32[]{:S(2)}) async-start(f32[1,4,64,128]{3,1,0,2:T(4,128)} %copy.36), calls=%async_computation | async-start | bytes 262144 | tf_op jit(solution)/shard_map/all_to_all | solution.py:122
  334.4 51.1 %all-gather.5.cloned.1.call-start = ((), (), s32[]{:S(2)}) async-start(), calls=%async_computation.3 | async-start | bytes 2228224 | tf_op jit(solution)/shard_map/all_gather | solution.py:144
Sparse Core Ops, SparseCore 0:
  345.3 40.0 all-gather.4
